TPU v7x, 32 devices: a whole 2x2x4 slice. The times are simulated.
32 devices in a mesh: fsdp: 8 (over z, core), tp: 4 (over y, x).
Axes of the slice: x: 2, y: 2, z: 4, core: 2. Of those that a mesh axis runs over, the one named last changes fastest.
Arguments:
- tokens: bfloat16 [80, 16384], P('tp', 'fsdp'), may hold values from -6 to 6
- gate_weight: bfloat16 [16384, 28672], P('fsdp', 'tp'), may hold values from -0.046875 to 0.046875
- up_weight: bfloat16 [16384, 28672], P('fsdp', 'tp'), may hold values from -0.046875 to 0.046875
- down_weight: bfloat16 [28672, 16384], P('tp', 'fsdp'), may hold values from -0.03125 to 0.03125
Outputs:
- layer_out: bfloat16 [80, 16384], P('tp', 'fsdp')
All inputs are finite; a program needn't handle non-finite values.
Results may differ from a plain program's by a relative error of at most 0.019.
Values may be sent and summed in bfloat16 or wider, within the bound.
A program may use at most 128 MiB of HBM per device.

v0:
```python
import jax
import jax.numpy as jnp
from jax import lax
from jax.sharding import PartitionSpec as P


def per_device(tokens, gate_weight, up_weight, down_weight):
    segment = lax.all_gather(tokens, "tp", axis=0, tiled=True)
    gate_part = jnp.dot(segment, gate_weight, preferred_element_type=jnp.float32)
    up_part = jnp.dot(segment, up_weight, preferred_element_type=jnp.float32)
    partials = jnp.stack([gate_part, up_part])
    summed = lax.psum_scatter(partials, "fsdp", scatter_dimension=2, tiled=True)
    hidden = (jax.nn.silu(summed[0]) * summed[1]).astype(jnp.bfloat16)
    outputs = jnp.dot(
        lax.all_gather(hidden, "fsdp", axis=1, tiled=True),
        down_weight,
        preferred_element_type=jnp.float32,
    )
    return lax.psum_scatter(outputs.astype(jnp.bfloat16), "tp", scatter_dimension=0, tiled=True)


def solution(mesh):
    placed = (P("tp", "fsdp"), P("fsdp", "tp"), P("fsdp", "tp"), P("tp", "fsdp"))
    return jax.shard_map(
        per_device, mesh=mesh, in_specs=placed, out_specs=P("tp", "fsdp"), check_vma=False
    )
```

profile of v0, /device:TPU:0, one launch (start us, length us, event | category | flops | bytes accessed | tf_op | source)
XLA Modules:
  0.0 188.8 jit_solution(4013773835530704543)
XLA Ops:
  6.5 0.0 reduce-scatter.2.cloned.1.call-start
  6.5 11.3 %all-gather = bf16[4,20,2048]{2,1,0:T(8,128)(2,1)S(1)} all-gather(bf16[1,20,2048]{2,1,0:T(8,128)(2,1)} %bitcast.22), channel_id=1, replica_groups=mesh['fsdp'=8,'tp'=4] {'tp'}, dimensions={0}, use_global_device_ids=true | all-gather | bytes 409600 | tf_op jit(solution)/shard_map/all_gather | solution.py:8
  17.9 0.1 reshape.1
  17.9 12.0 %convolution_bitcast_fusion = f32[1,80,7168]{2,1,0:T(8,128)S(1)} fusion(bf16[80,2048]{1,0:T(8,128)(2,1)S(1)} %reshape.1, bf16[2048,7168]{1,0:T(8,128)(2,1)} %param.6), kind=kOutput, calls=%fused_computation | convolution fusion | flops 2348810240 | bytes 31981568 | tf_op jit(solution)/shard_map/dot_general | solution.py:10
  29.9 12.0 %convolution_bitcast_fusion.1 = f32[1,80,7168]{2,1,0:T(8,128)S(1)} fusion(bf16[80,2048]{1,0:T(8,128)(2,1)S(1)} %reshape.1, bf16[2048,7168]{1,0:T(8,128)(2,1)} %param.5), kind=kOutput, calls=%fused_computation.1 | convolution fusion | flops 2348810240 | bytes 31981568 | tf_op jit(solution)/shard_map/dot_general | solution.py:9
  42.0 2.4 %pad_maximum_fusion = f32[2,80,7168]{2,1,0:T(8,128)} fusion(f32[1,80,7168]{2,1,0:T(8,128)S(1)} %convolution_bitcast_fusion, f32[1,80,7168]{2,1,0:T(8,128)S(1)} %convolution_bitcast_fusion.1), kind=kLoop, calls=%fused_computation.2 | loop fusion | flops 1146880 | bytes 9175040 | tf_op jit(solution)/shard_map/stack | solution.py:11
  44.3 0.0 reduce-scatter.2.cloned.1.call-update
  44.4 0.0 all-gather.3.cloned.1.call-start
  44.4 54.0 %reduce-scatter.2.cloned.1.call-done = f32[2,80,896]{2,1,0:T(8,128)} async-done(((f32[2,80,7168]{2,1,0:T(8,128)}), f32[2,80,896]{2,1,0:T(8,128)}) %reduce-scatter.2.cloned.1.call-update) | async-done | bytes 573456 | tf_op jit(solution)/shard_map/reduce_scatter | solution.py:12
  98.4 1.8 fusion.1
  100.2 0.0 all-gather.3.cloned.1.call-update
  100.2 0.0 copy-start
  100.2 0.0 all-reduce.3.cloned.1.call-start
  100.3 21.4 %all-gather.3.cloned.1.call-done = bf16[80,7168]{1,0:T(8,128)(2,1)} async-done(((bf16[80,896]{1,0:T(8,128)(2,1)}), bf16[80,7168]{1,0:T(8,128)(2,1)}) %all-gather.3.cloned.1.call-update) | async-done | bytes 1146896 | tf_op jit(solution)/shard_map/all_gather | solution.py:15
  121.7 15.6 %convolution_convert_fusion = bf16[80,2048]{1,0:T(8,128)(2,1)} fusion(bf16[80,7168]{1,0:T(8,128)(2,1)} %all-gather.3.cloned.1.call-done, bf16[7168,2048]{1,0:T(8,128)(2,1)} %param.7), kind=kOutput, calls=%fused_computation.3 | convolution fusion | flops 2348974080 | bytes 30834688 | tf_op jit(solution)/shard_map/dot_general | solution.py:14
  137.3 0.0 all-reduce.3.cloned.1.call-update
  137.3 0.0 copy-done
  137.3 0.6 dynamic-slice
  138.6 42.1 %all-reduce.3.cloned.1.call-done = bf16[80,2048]{1,0:T(8,128)(2,1)} async-done(((bf16[80,2048]{1,0:T(8,128)(2,1)}), bf16[80,2048]{1,0:T(8,128)(2,1)}) %all-reduce.3.cloned.1.call-update) | async-done | bytes 327696
  180.7 1.6 constant_dynamic-slice_fusion
Async XLA Ops:
  6.5 91.9 %reduce-scatter.2.cloned.1.call-start = ((), (), s32[]{:S(2)}) async-start(), calls=%async_computation.1 | async-start | bytes 5160960 | tf_op jit(solution)/shard_map/reduce_scatter | solution.py:12
  44.4 77.3 %all-gather.3.cloned.1.call-start = ((), (), s32[]{:S(2)}) async-start(), calls=%async_computation.2 | async-start | bytes 1290240 | tf_op jit(solution)/shard_map/all_gather | solution.py:15
  100.2 37.1 %copy-start = (u32[32]{0:T(128)S(1)}, u32[32]{0:T(128)}, u32[]{:S(2)}) copy-start(u32[32]{0:T(128)} %constant.5) | copy-start | bytes 388
  100.2 80.4 %all-reduce.3.cloned.1.call-start = ((), (), s32[]{:S(2)}) async-start(), calls=%async_computation.3 | async-start | bytes 655360
Sparse Core Ops, SparseCore 0:
  44.5 53.8 reduce-scatter.1
  100.3 21.2 all-gather.2
  137.4 43.1 all-reduce.2
where the time goes:
time: 189 us
  waiting for transfers between devices  118 us (62%)
  matrix products  39.6 us (21%)
  between operations  13.8 us (7%)
  blocking collectives  11.3 us (6%)
  other arithmetic  4.16 us (2%)
  local copies, waits for them, and re-layouts  2.23 us (1%)
    reduce_scatter x1, waiting for transfers between devices, per_device(): summed = lax.psum_scatter(partials, 'fsdp', scatter_dimension=2, tiled=True)  54 us
    unnamed x4, waiting for transfers between devices  42.2 us
    all_gather x1, waiting for transfers between devices, per_device(): lax.all_gather(hidden, 'fsdp', axis=1, tiled=True)  21.4 us
    dot_general x1, matrix products, per_device(): jnp.dot(lax.all_gather(hidden, 'fsdp', axis=1, tiled=True), down_weight,...  15.6 us
    dot_general x1, matrix products, per_device(): up_part = jnp.dot(segment, up_weight, preferred_element_type=jnp.float32)  12 us
    dot_general x1, matrix products, per_device(): jnp.dot(segment, gate_weight, preferred_element_type=jnp.float32)  12 us
    all_gather x1, blocking collectives, per_device(): segment = lax.all_gather(tokens, 'tp', axis=0, tiled=True)  11.3 us
  transfers between devices with their start and end apart: 3, of which 3 were waited for; matrix products, arithmetic and copies ran while one was open for 0% of the time, Pallas kernels for 0%

commit v1 on v0

v1 whole, which is shorter than its diff:
```python
import functools

import jax
import jax.numpy as jnp
from jax import lax
from jax.experimental import pallas as pl
from jax.experimental.pallas import tpu as pltpu
from jax.sharding import PartitionSpec as P

MESH = pl.DeviceIdType.MESH
F32, BF16 = jnp.float32, jnp.bfloat16
LANES, PACK = 128, 16
VMEM_LIMIT = 66_000_000


def placing(shape, rows, padded, parts, along):
    wide = lax.broadcasted_iota(jnp.int32, shape, along)
    tight = lax.broadcasted_iota(jnp.int32, shape, 1 - along)
    hit = jnp.zeros(shape, F32)
    for part in range(parts):
        here = (tight >= part * rows) & (tight < (part + 1) * rows)
        hit = jnp.where(here & (wide - part * padded == tight - part * rows), 1.0, hit)
    return hit.astype(BF16)


def kernel(F, T, R, tok, gate, up, down, out, gath, seg, wbuf, dn, part, pin, red, zin, hall, acc, obuf, oin,
           wsem, dsem, tsend, trecv, psend, precv, zsend, zrecv, hsend, hrecv, fsend, frecv, osend, orecv):
    Z = F // 2
    RP, DL = tok.shape
    K, W = hall.shape[0], F * LANES
    half = Z * LANES
    f, t = lax.axis_index("fsdp"), lax.axis_index("tp")
    z, c = f // 2, f % 2
    partner = z * 2 + (1 - c)
    place = c * Z + z

    def chip(o):
        return lax.rem(z + o, Z) * 2 + c

    def peer(o):
        return lax.rem(t + o, T)

    def remote(src, dst, send, recv, where):
        return pltpu.make_async_remote_copy(src_ref=src, dst_ref=dst, send_sem=send, recv_sem=recv,
                                            device_id=where, device_id_type=MESH)

    def weights(k):
        slot = lax.rem(k, 2)
        cols = pl.ds(pl.multiple_of(k * W, W), W)
        return [pltpu.make_async_copy(w.at[:, cols], wbuf.at[slot, i], wsem.at[slot, i]) for i, w in enumerate((gate, up))]

    def downs(k):
        return pltpu.make_async_copy(down.at[pl.ds(pl.multiple_of(k * W, W), W), :], dn.at[k], dsem.at[k])

    def pair(k):
        return remote(part.at[k, 1 - c], pin.at[k], psend.at[k], precv.at[k], {"fsdp": partner})

    def across(k, o):
        return remote(red.at[k, lax.rem(z + o, Z)], zin.at[k, o - 1], zsend.at[k, o - 1], zrecv.at[k, o - 1], {"fsdp": chip(o)})

    def spread(k, o):
        return remote(hall.at[k, place], hall.at[k, place], hsend.at[k, o - 1], hrecv.at[k, o - 1], {"fsdp": chip(o)})

    def forward(k):
        mine = pl.ds(c * Z, Z)
        return remote(hall.at[k, mine], hall.at[k, mine], fsend.at[k], frecv.at[k], {"fsdp": partner})

    def tokens(o):
        return remote(tok, gath.at[t], tsend.at[o - 1], trecv.at[o - 1], {"tp": peer(o)})

    def result(o):
        return remote(obuf.at[peer(o)], oin.at[o - 1], osend.at[o - 1], orecv.at[o - 1], {"tp": peer(o)})

    for k in range(min(2, K)):
        for copy in weights(k):
            copy.start()

    barrier = pltpu.get_barrier_semaphore()
    pl.semaphore_signal(barrier, inc=1, device_id={"fsdp": partner}, device_id_type=MESH)
    for o in range(1, Z):
        pl.semaphore_signal(barrier, inc=1, device_id={"fsdp": chip(o)}, device_id_type=MESH)
    for o in range(1, T):
        pl.semaphore_signal(barrier, inc=1, device_id={"tp": peer(o)}, device_id_type=MESH)
    pl.semaphore_wait(barrier, 1 + (Z - 1) + (T - 1))

    for o in range(1, T):
        tokens(o).start()
    gath[t] = tok[...]
    acc[...] = jnp.zeros_like(acc)
    for o in range(1, T):
        tokens(o).wait()
    seg[...] = jnp.dot(placing((T * R, T * RP), R, RP, T, 1), gath[...].reshape(T * RP, DL),
                       preferred_element_type=F32).astype(BF16)

    def step(k, carry):
        @pl.when(k < K)
        def _():
            slot = lax.rem(k, 2)
            for copy in weights(k):
                copy.wait()
            for i in range(2):
                for h in range(2):
                    part[k, h, i] = jnp.dot(seg[...], wbuf[slot, i, :, h * half:(h + 1) * half],
                                            preferred_element_type=F32).astype(BF16)
            pair(k).start()

            @pl.when(k + 2 < K)
            def _():
                for copy in weights(k + 2):
                    copy.start()

            @pl.when(k == max(K - 2, 0))
            def _():
                for j in range(K):
                    downs(j).start()

        @pl.when((k >= 1) & (k - 1 < K))
        def _():
            j = k - 1
            pair(j).wait_recv()
            for i in range(2):
                both = part[j, c, i].astype(F32) + pin[j, i].astype(F32)
                for zz in range(Z):
                    red[j, zz, i] = both[:, zz * LANES:(zz + 1) * LANES].astype(BF16)
            for o in range(1, Z):
                across(j, o).start()

        @pl.when((k >= 3) & (k - 3 < K))
        def _():
            j = k - 3
            sums = [red[j, z, i].astype(F32) for i in range(2)]
            for o in range(1, Z):
                across(j, o).wait_recv()
                sums = [sums[i] + zin[j, o - 1, i].astype(F32) for i in range(2)]
            g, u = sums
            hall[j, place] = (g / (1.0 + jnp.exp(-g)) * u).astype(BF16)
            for o in range(1, Z):
                spread(j, o).start()

        @pl.when((k >= 5) & (k - 5 < K))
        def _():
            j = k - 5
            for o in range(1, Z):
                spread(j, o).wait_recv()
            forward(j).start()

        @pl.when((k >= 6) & (k - 6 < K))
        def _():
            j = k - 6
            downs(j).wait()
            forward(j).wait_recv()
            hidden = jnp.concatenate([hall[j, p] for p in range(F)], axis=1)
            span = 512 if DL % 512 == 0 else LANES
            for n in range(0, DL, span):
                acc[:, n:n + span] += jnp.dot(hidden, dn[j, :, n:n + span], preferred_element_type=F32)

        return carry

    lax.fori_loop(0, K + 6, step, 0)

    obuf[...] = jnp.dot(placing((T * RP, T * R), R, RP, T, 0), acc[...].astype(BF16),
                        preferred_element_type=F32).astype(BF16).reshape(T, RP, DL)
    for o in range(1, T):
        result(o).start()

    def drain(k, carry):
        pair(k).wait_send()
        forward(k).wait_send()
        for o in range(1, Z):
            across(k, o).wait_send()
            spread(k, o).wait_send()
        return carry

    lax.fori_loop(0, K, drain, 0)
    total = obuf[t].astype(F32)
    for o in range(1, T):
        result(o).wait()
        total = total + oin[o - 1].astype(F32)
    out[...] = total.astype(BF16)[:R]


def fused(F, T, tokens, gate_weight, up_weight, down_weight):
    R, DL = tokens.shape
    FL = gate_weight.shape[1]
    RP = -(-R // PACK) * PACK
    W, Z, M = F * LANES, F // 2, T * R
    K = FL // W
    padded = jnp.pad(tokens, ((0, RP - R), (0, 0)))
    dma = pltpu.SemaphoreType.DMA
    vmem = pltpu.VMEM
    flops = 2 * M * DL * FL * 3
    return pl.pallas_call(
        functools.partial(kernel, F, T, R),
        out_shape=jax.ShapeDtypeStruct((R, DL), BF16),
        in_specs=[pl.BlockSpec(memory_space=pltpu.VMEM)] + [pl.BlockSpec(memory_space=pl.ANY)] * 3,
        out_specs=pl.BlockSpec(memory_space=pltpu.VMEM),
        scratch_shapes=[
            vmem((T, RP, DL), BF16), vmem((M, DL), BF16),
            vmem((2, 2, DL, W), BF16), vmem((K, W, DL), BF16),
            vmem((K, 2, 2, M, Z * LANES), BF16), vmem((K, 2, M, Z * LANES), BF16),
            vmem((K, Z, 2, M, LANES), BF16), vmem((K, Z - 1, 2, M, LANES), BF16),
            vmem((K, F, M, LANES), BF16), vmem((M, DL), F32),
            vmem((T, RP, DL), BF16), vmem((T - 1, RP, DL), BF16),
            dma((2, 2)), dma((K,)), dma((T - 1,)), dma((T - 1,)), dma((K,)), dma((K,)),
            dma((K, Z - 1)), dma((K, Z - 1)), dma((K, Z - 1)), dma((K, Z - 1)),
            dma((K,)), dma((K,)), dma((T - 1,)), dma((T - 1,)),
        ],
        compiler_params=pltpu.CompilerParams(collective_id=0, has_side_effects=True, vmem_limit_bytes=VMEM_LIMIT),
        cost_estimate=pl.CostEstimate(flops=flops, bytes_accessed=6 * DL * FL, transcendentals=0),
        name="swiglu_block",
    )(padded, gate_weight, up_weight, down_weight)


def per_device(F, T, tokens, gate_weight, up_weight, down_weight):
    DL, FL = gate_weight.shape
    held = 2 * (FL * DL + 4 * DL * F * LANES)
    if F % 4 == 0 and T > 1 and FL % (F * LANES) == 0 and DL % LANES == 0 and held < VMEM_LIMIT - 2**23:
        return fused(F, T, tokens, gate_weight, up_weight, down_weight)
    segment = lax.all_gather(tokens, "tp", axis=0, tiled=True)
    gate_part = jnp.dot(segment, gate_weight, preferred_element_type=F32)
    up_part = jnp.dot(segment, up_weight, preferred_element_type=F32)
    partials = jnp.stack([gate_part, up_part])
    summed = lax.psum_scatter(partials, "fsdp", scatter_dimension=2, tiled=True)
    hidden = (jax.nn.silu(summed[0]) * summed[1]).astype(BF16)
    outputs = jnp.dot(lax.all_gather(hidden, "fsdp", axis=1, tiled=True), down_weight, preferred_element_type=F32)
    return lax.psum_scatter(outputs.astype(BF16), "tp", scatter_dimension=0, tiled=True)


def solution(mesh):
    placed = (P("tp", "fsdp"), P("fsdp", "tp"), P("fsdp", "tp"), P("tp", "fsdp"))
    return jax.shard_map(
        functools.partial(per_device, mesh.shape["fsdp"], mesh.shape["tp"]),
        mesh=mesh, in_specs=placed, out_specs=P("tp", "fsdp"), check_vma=False,
    )
```

time: 189 us -> 72.2 us (0.38)
  waiting for transfers between devices: 118 us -> 0 us
  Pallas kernels: 0 us -> 68.9 us
  matrix products: 39.6 us -> 0 us
  between operations: 13.8 us -> 0.01 us
  blocking collectives: 11.3 us -> 0 us
  other arithmetic: 4.16 us -> 0 us
    pallas_call x0 -> x1, Pallas kernels: none -> 68.9 us  [fused(): pl.pallas_call(functools.partial(kernel, F, T, R), out_shape=jax.ShapeDty...]
    reduce_scatter x1 -> x0, waiting for transfers between devices: 54 us -> none  [per_device(): summed = lax.psum_scatter(partials, 'fsdp', scatter_dimension=2, tiled=True)]
    unnamed x4 -> x0, waiting for transfers between devices: 42.2 us -> none
    dot_general x3 -> x0, matrix products: 39.6 us -> none  [the longest x1 15.6 us: per_device(): jnp.dot(lax.all_gather(hidden, 'fsdp', axis=1, tiled=True), down_weight,...]
    all_gather x1 -> x0, waiting for transfers between devices: 21.4 us -> none  [per_device(): lax.all_gather(hidden, 'fsdp', axis=1, tiled=True)]
    all_gather x1 -> x0, blocking collectives: 11.3 us -> none  [per_device(): segment = lax.all_gather(tokens, 'tp', axis=0, tiled=True)]
    another operation x1 -> x0, other arithmetic: 2.37 us -> none  [per_device(): partials = jnp.stack([gate_part, up_part])]
  transfers between devices with their start and end apart: 3 -> 0, of which waited for: 3 -> 0; matrix products, arithmetic and copies ran while one was open for 0% -> 0% of each run, Pallas kernels for 0% -> 0%
where the time goes in v1:
time: 72.2 us; the launch traced here: 72 us
  Pallas kernels  68.9 us (95%)
  local copies, waits for them, and re-layouts  3.08 us (4%)
    pallas_call x1, Pallas kernels, fused(): pl.pallas_call(functools.partial(kernel, F, T, R), out_shape=jax.ShapeDty...  68.9 us
    unnamed x1, local copies, waits for them, and re-layouts  1.54 us
    pad x1, local copies, waits for them, and re-layouts, fused(): padded = jnp.pad(tokens, ((0, RP - R), (0, 0)))  1.54 us

profile of v1, /device:TPU:0, one launch (start us, length us, event | category | flops | bytes accessed | tf_op | source)
XLA Modules:
  0.0 72.0 jit_solution(13549272081950173968)
XLA Ops:
  0.0 1.5 %pad.4.tok = bf16[32,2048]{1,0:T(8,128)(2,1)} pad(bf16[20,2048]{1,0:T(8,128)(2,1)} %param.4, bf16[]{:T(256)} %constant.2.clone.1), padding=0_12x0_0 | pad | bytes 212994 | tf_op jit(solution)/shard_map/jit(_pad)/pad | solution.py:188
  1.5 68.9 %swiglu_block.1 = bf16[20,2048]{1,0:T(8,128)(2,1)} custom-call(bf16[32,2048]{1,0:T(8,128)(2,1)} %pad.4.tok, bf16[2048,7168]{1,0:T(8,128)(2,1)} %gate.1, bf16[2048,7168]{1,0:T(8,128)(2,1)} %up.1, bf16[7168,2048]{1,0:T(8,128)(2,1)} %down.1), custom_call_target="tpu_custom_call" | custom-call | flops 7046430720 | bytes 88080384 | tf_op jit(solution)/shard_map/swiglu_block/pallas_call | solution.py:192
  70.4 1.5 %copy.6 = bf16[20,2048]{1,0:T(8,128)(2,1)} copy(bf16[20,2048]{1,0:T(8,128)(2,1)} %swiglu_block.1) | data formatting | bytes 163840
